TPU v7x, 128 devices: a whole 4x4x4 slice. The times are simulated.
128 devices in a mesh: gx: 16 (over y, x_lo, core), gy: 8 (over z, x_hi).
Axes of the slice: x: 4 (x_hi: 2, x_lo: 2; x = x_hi * 2 + x_lo), y: 4, z: 4, core: 2. Of those that a mesh axis runs over, the one named last changes fastest.
Arguments:
- thinker_normed: bfloat16 [8, 16, 8192], P(None, None, 'gx'), may hold values from -6 to 6
- thinker_resid: bfloat16 [8, 16, 8192], P('gy', None, 'gx'), may hold values from -6 to 6
- gate_weight: bfloat16 [8192, 29568], P('gx', 'gy'), may hold values from -0.0625 to 0.0625
- up_weight: bfloat16 [8192, 29568], P('gx', 'gy'), may hold values from -0.0625 to 0.0625
- down_weight: bfloat16 [29568, 8192], P('gy', 'gx'), may hold values from -0.03125 to 0.03125
- bridge_weight: bfloat16 [8192, 3584], P('gx'), may hold values from -0.0625 to 0.0625
- talker_stream: bfloat16 [8, 3072, 3584], P('gy', 'gx'), may hold values from -6 to 6
- norm_gain: float32 [3584], replicated, may hold values from 0.5 to 2
- w_query: bfloat16 [3584, 1792], P(None, 'gy'), may hold values from -0.09375 to 0.09375
- w_key: bfloat16 [3584, 256], P(None, 'gy'), may hold values from -0.09375 to 0.09375
- w_value: bfloat16 [3584, 256], P(None, 'gy'), may hold values from -0.09375 to 0.09375
- a_query: bfloat16 [3584, 64], replicated, may hold values from -0.09375 to 0.09375
- b_query: bfloat16 [64, 1792], replicated, may hold values from -0.75 to 0.75
- a_value: bfloat16 [3584, 64], replicated, may hold values from -0.09375 to 0.09375
- b_value: bfloat16 [64, 256], replicated, may hold values from -0.75 to 0.75
- text_index: int32 [8, 3072], P('gy', 'gx'), may hold values from 0 to 15
- span_offset: int32 [8], P('gy'), may hold values from 1 to 3071
- out_grad: bfloat16 [8, 3072, 1792], P('gy', 'gx'), may hold values from -6 to 6
Outputs:
- attn_out: bfloat16 [8, 3072, 1792], P('gy', 'gx')
- grad_aq: float32 [3584, 64], replicated
- grad_bq: float32 [64, 1792], replicated
- grad_av: float32 [3584, 64], replicated
- grad_bv: float32 [64, 256], replicated
All inputs are finite; a program needn't handle non-finite values.
Results may differ from a plain program's by a relative error of at most 0.035.
Values may be sent and summed in bfloat16 or wider, within the bound.
A program may use at most 192 MiB of HBM per device.

v0:
```python
import math
import jax
import jax.numpy as jnp
from jax import lax
from jax.sharding import PartitionSpec as P

HEADS = 14
KVH = 2
HD = 128
rope_base = 1000000.0
norm_eps = 1e-06


def cut_along(array, dim, size):
    dims = array.shape
    parts = array.reshape(*dims[:dim], size, dims[dim] // size, *dims[dim + 1 :])
    return jnp.moveaxis(parts, dim, 0)


def sent_and_summed(array, axis, dim):
    size = lax.axis_size(axis)
    parts = lax.all_to_all(cut_along(array, dim, size), axis, 0, 0, tiled=True)
    return jnp.sum(parts, axis=0)


def angle_tables(first_pos, length):
    position = (first_pos + jnp.arange(length, dtype=jnp.int32)).astype(jnp.float32)
    frequency = rope_base ** (-(2.0 * jnp.arange(HD // 2, dtype=jnp.float32)) / HD)
    angles = position[:, None] * frequency[None, :]
    return (jnp.cos(angles), jnp.sin(angles))


def rotate(tensor, cosine, sine_table, signed):
    layout = (cosine.shape[0],) + (1,) * (tensor.ndim - 2) + (cosine.shape[1],)
    cosine = cosine.reshape(layout)
    sine_part = sine_table.reshape(layout) * signed
    half_width = tensor.shape[-1] // 2
    first_half = tensor[..., :half_width]
    second_half = tensor[..., half_width:]
    return jnp.concatenate(
        [
            first_half * cosine - second_half * sine_part,
            second_half * cosine + first_half * sine_part,
        ],
        axis=-1,
    )


def on_device(
    thinker_normed,
    thinker_resid,
    gate_weight,
    up_weight,
    down_weight,
    bridge_weight,
    talker_stream,
    norm_gain,
    w_query,
    w_key,
    w_value,
    a_query,
    b_query,
    a_value,
    b_value,
    text_index,
    span_offset,
    out_grad,
):
    seq_count, rows_seq, columns = thinker_normed.shape
    normed = thinker_normed.reshape(seq_count * rows_seq, columns)
    ff_local = gate_weight.shape[1]
    block = normed
    gate_part = jnp.dot(block, gate_weight, preferred_element_type=jnp.float32)
    up_part = jnp.dot(block, up_weight, preferred_element_type=jnp.float32)
    both_parts = sent_and_summed(jnp.concatenate([gate_part, up_part], axis=1), "gx", 0)
    hidden = (jax.nn.silu(both_parts[:, :ff_local]) * both_parts[:, ff_local:]).astype(jnp.bfloat16)
    partial_out = jnp.dot(
        lax.all_gather(hidden, "gx", axis=0, tiled=True),
        down_weight,
        preferred_element_type=jnp.float32,
    )
    summed = sent_and_summed(partial_out, "gy", 0)
    thinker_out = (summed + thinker_resid[0].astype(jnp.float32)).astype(jnp.bfloat16)
    bridge_part = jnp.dot(thinker_out, bridge_weight, preferred_element_type=jnp.float32)
    bridge = lax.psum(bridge_part, "gx").astype(jnp.bfloat16)
    tokens = talker_stream.shape[1]
    groups = HEADS // KVH
    scale = 1.0 / math.sqrt(HD)
    picks = (text_index[0][:, None] == jnp.arange(rows_seq, dtype=jnp.int32)[None, :]).astype(
        jnp.bfloat16
    )
    mixed = talker_stream[0].astype(jnp.float32) + jnp.dot(
        picks, bridge, preferred_element_type=jnp.float32
    )
    normal = (
        mixed * lax.rsqrt(jnp.mean(mixed * mixed, axis=1, keepdims=True) + norm_eps) * norm_gain
    ).astype(jnp.bfloat16)
    low_query = jnp.dot(normal, a_query, preferred_element_type=jnp.float32).astype(jnp.bfloat16)
    low_value = jnp.dot(normal, a_value, preferred_element_type=jnp.float32).astype(jnp.bfloat16)
    slab_rows = lax.all_gather(normal, "gy", axis=0, tiled=True)
    projected = jnp.concatenate(
        [
            jnp.dot(slab_rows, w_query, preferred_element_type=jnp.float32),
            jnp.dot(slab_rows, w_key, preferred_element_type=jnp.float32),
            jnp.dot(slab_rows, w_value, preferred_element_type=jnp.float32),
        ],
        axis=1,
    )
    returned = lax.all_to_all(projected, "gy", split_axis=0, concat_axis=1, tiled=True)
    parcels = returned.reshape(tokens, lax.axis_size("gy"), -1)
    query_cols = w_query.shape[1]
    key_cols = w_key.shape[1]
    base_query = parcels[:, :, :query_cols].reshape(tokens, -1)
    base_key = parcels[:, :, query_cols : query_cols + key_cols].reshape(tokens, -1)
    base_value = parcels[:, :, query_cols + key_cols :].reshape(tokens, -1)
    first_pos = lax.axis_index("gx") * tokens
    cosine, sine_table = angle_tables(first_pos, tokens)
    query_pre = base_query + jnp.dot(low_query, b_query, preferred_element_type=jnp.float32)
    query = rotate(query_pre.reshape(tokens, KVH, groups, HD), cosine, sine_table, 1.0).astype(
        jnp.bfloat16
    )
    key_local = (
        rotate(base_key.reshape(tokens, KVH, HD), cosine, sine_table, 1.0)
        .astype(jnp.bfloat16)
        .reshape(tokens, KVH * HD)
    )
    value_local = (
        base_value + jnp.dot(low_value, b_value, preferred_element_type=jnp.float32)
    ).astype(jnp.bfloat16)
    key_all, value_all = (
        lax.all_gather(key_local, "gx", axis=0, tiled=True),
        lax.all_gather(value_local, "gx", axis=0, tiled=True),
    )
    length = key_all.shape[0]
    key_rows = key_all.reshape(length, KVH, HD)
    value_rows = value_all.reshape(length, KVH, HD)
    query_places = first_pos + jnp.arange(tokens, dtype=jnp.int32)
    key_places = jnp.arange(length, dtype=jnp.int32)
    causal = (key_places[None, :] <= query_places[:, None]) | (key_places[None, :] < span_offset[0])
    scores = (
        jnp.einsum("tkgd,skd->kgts", query, key_rows, preferred_element_type=jnp.float32) * scale
    )
    scores = jnp.where(causal, scores, -1e30)
    row_max = jnp.max(scores, axis=-1, keepdims=True)
    weights = jnp.exp(scores - row_max)
    probs = (weights / jnp.sum(weights, axis=-1, keepdims=True)).astype(jnp.bfloat16)
    attended = jnp.einsum(
        "kgts,skd->tkgd", probs, value_rows, preferred_element_type=jnp.float32
    ).astype(jnp.bfloat16)
    grad_four = out_grad[0].reshape(tokens, KVH, groups, HD)
    inner_prod = jnp.sum(grad_four.astype(jnp.float32) * attended.astype(jnp.float32), axis=-1)
    dprob = jnp.einsum("tkgd,skd->kgts", grad_four, value_rows, preferred_element_type=jnp.float32)
    dscore = (
        probs.astype(jnp.float32) * (dprob - jnp.transpose(inner_prod, (1, 2, 0))[..., None])
    ).astype(jnp.bfloat16)
    dquery = (
        jnp.einsum("kgts,skd->tkgd", dscore, key_rows, preferred_element_type=jnp.float32) * scale
    )
    query_grad = (
        rotate(dquery, cosine, sine_table, -1.0).reshape(tokens, HEADS * HD).astype(jnp.bfloat16)
    )
    block = probs
    term = jnp.einsum("kgts,tkgd->skd", block, grad_four, preferred_element_type=jnp.float32)
    value_grad = sent_and_summed(
        term.reshape(tokens * lax.axis_size("gx"), KVH * HD), "gx", 0
    ).astype(jnp.bfloat16)
    part_bq = jnp.einsum("tr,tc->rc", low_query, query_grad, preferred_element_type=jnp.float32)
    part_bv = jnp.einsum("tr,tc->rc", low_value, value_grad, preferred_element_type=jnp.float32)
    dlow_query = jnp.einsum(
        "tc,rc->tr", query_grad, b_query, preferred_element_type=jnp.float32
    ).astype(jnp.bfloat16)
    dlow_value = jnp.einsum(
        "tc,rc->tr", value_grad, b_value, preferred_element_type=jnp.float32
    ).astype(jnp.bfloat16)
    part_aq = jnp.einsum("td,tr->dr", normal, dlow_query, preferred_element_type=jnp.float32)
    part_av = jnp.einsum("td,tr->dr", normal, dlow_value, preferred_element_type=jnp.float32)
    grad_aq, grad_bq, grad_av, grad_bv = lax.psum(
        (part_aq, part_bq, part_av, part_bv), ("gx", "gy")
    )
    attn_out = attended.reshape(1, tokens, HEADS * HD)
    return (attn_out, grad_aq, grad_bq, grad_av, grad_bv)


def solution(mesh):
    return jax.shard_map(
        on_device,
        mesh=mesh,
        in_specs=(
            P(None, None, "gx"),
            P("gy", None, "gx"),
            P("gx", "gy"),
            P("gx", "gy"),
            P("gy", "gx"),
            P("gx", None),
            P("gy", "gx", None),
            P(),
            P(None, "gy"),
            P(None, "gy"),
            P(None, "gy"),
            P(),
            P(),
            P(),
            P(),
            P("gy", "gx"),
            P("gy"),
            P("gy", "gx", None),
        ),
        out_specs=(P("gy", "gx", None), P(), P(), P(), P()),
        check_vma=False,
    )
```

profile of v0, /device:TPU:1, one launch (start us, length us, event | category | flops | bytes accessed | tf_op | source)
XLA Modules:
  0.0 656.2 jit_solution(4535558930171179902)
XLA Ops:
  7.2 3.4 fusion.59
  13.9 5.3 copy.44
  19.2 52.4 %all_to_all.31 = f32[16,8,7392]{2,1,0:T(8,128)} all-to-all(f32[16,8,7392]{2,1,0:T(8,128)} %bitcast.99), channel_id=1, replica_groups=mesh['gx'=16,'gy'=8] {'gx'}, dimensions={0} | all-to-all | bytes 7569408 | tf_op jit(solution)/shard_map/all_to_all | solution.py:22
  74.0 21.7 %all_gather.12 = bf16[128,3696]{1,0:T(8,128)(2,1)S(1)} all-gather(bf16[8,3696]{1,0:T(8,128)(2,1)S(1)} %fusion.37), channel_id=1, replica_groups=mesh['gx'=16,'gy'=8] {'gx'}, dimensions={0}, use_global_device_ids=true | all-gather | bytes 1005312 | tf_op jit(solution)/shard_map/all_gather | solution.py:78
  98.5 15.4 %all_to_all.32 = f32[8,16,512]{2,1,0:T(8,128)S(1)} all-to-all(f32[8,16,512]{2,1,0:T(8,128)S(1)} %bitcast.105), channel_id=1, replica_groups=mesh['gx'=16,'gy'=8] {'gy'}, dimensions={0} | all-to-all | bytes 524288 | tf_op jit(solution)/shard_map/all_to_all | solution.py:22
  116.7 52.2 %all-reduce.5 = bf16[16,3584]{1,0:T(8,128)(2,1)S(1)} all-reduce(f32[16,3584]{1,0:T(8,128)S(1)} %fusion.46), channel_id=1, replica_groups=mesh['gx'=16,'gy'=8] {'gx'}, use_global_device_ids=true, to_apply=%region_2.3 | all-reduce | flops 57344 | bytes 344064 | tf_op jit(solution)/shard_map/psum | solution.py:85
  171.1 128.6 %all-gather.4.cloned.1.call-done = bf16[1536,3584]{1,0:T(8,128)(2,1)} async-done(((bf16[192,3584]{1,0:T(8,128)(2,1)}), bf16[1536,3584]{1,0:T(8,128)(2,1)}) %all-gather.4.cloned.1.call-update) | async-done | bytes 11010064 | tf_op jit(solution)/shard_map/all_gather | solution.py:100
  299.7 7.2 %fusion.62 = f32[1536,224]{0,1:T(8,128)S(1)} fusion(bf16[1536,3584]{1,0:T(8,128)(2,1)} %all-gather.4.cloned.1.call-done, bf16[3584,224]{0,1:T(8,128)(2,1)S(1)} %copy-done), kind=kOutput, calls=%fused_computation.82 | convolution fusion | flops 2466250752 | bytes 13991936 | tf_op jit(solution)/shard_map/dot_general | solution.py:103
  307.0 3.3 fusion.63
  310.3 3.3 fusion.64
  315.8 3.9 copy.45
  319.7 4.4 all-to-all-start.2
  324.8 29.3 %all-to-all-done.2 = f32[8,192,288]{1,2,0:T(8,128)} async-done(((f32[8,192,288]{1,2,0:T(8,128)}), f32[8,192,288]{1,2,0:T(8,128)}, u32[]{:S(2)}, u32[]{:S(2)}) %all-to-all-start.2) | async-done | bytes 1769504 | tf_op jit(solution)/shard_map/all_to_all | solution.py:109
  375.3 13.8 %all-gather.8.cloned.1.call-done = bf16[3072,256]{1,0:T(8,128)(2,1)} async-done(((bf16[192,256]{1,0:T(8,128)(2,1)}), bf16[3072,256]{1,0:T(8,128)(2,1)}) %all-gather.8.cloned.1.call-update) | async-done | bytes 1572880 | tf_op jit(solution)/shard_map/all_gather | solution.py:131
  390.8 19.7 %fusion.58 = (f32[2,7,192]{2,1,0:T(8,128)S(1)}, f32[2,7,192,3072]{3,2,1,0:T(8,128)}) fusion(bf16[3072,2,128,1]{0,2,3,1:T(8,128)(2,1)S(1)} %bitcast.103, pred[192,3072]{1,0:T(8,128)(4,1)} %fusion.14, bf16[192,2,7,64]{3,0,2,1:T(8,128)(2,1)} %get-tuple-element.10, bf16[192,2,7,64]{3,0,2,1:T(8,128)(2,1)} %get-tuple-element.9), kind=kOutput, calls=%fused_computation.78 | convolution fusion | flops 2148338688 | bytes 35891712 | tf_op jit(solution)/shard_map/sub | solution.py:145
  410.5 13.3 %divide_convert_fusion = bf16[2,7,192,3072]{3,2,1,0:T(8,128)(2,1)S(1)} fusion(f32[2,7,192,3072]{3,2,1,0:T(8,128)} %get-tuple-element.25, f32[2,7,192]{2,1,0:T(8,128)S(1)} %get-tuple-element.24), kind=kLoop, calls=%fused_computation.5 | loop fusion | flops 16515072 | bytes 49555968 | tf_op jit(solution)/shard_map/convert_element_type | solution.py:146
  423.9 8.7 %convolution_bitcast_fusion = f32[3072,2,128]{2,0,1:T(8,128)} fusion(bf16[2,7,192,3072]{3,2,1,0:T(8,128)(2,1)S(1)} %divide_convert_fusion, bf16[192,2,7,128]{3,2,1,0:T(8,128)(2,1)S(1)} %copy-done.6), kind=kOutput, calls=%fused_computation.16 | convolution fusion | flops 2113929216 | bytes 20348928 | tf_op jit(solution)/shard_map/kgts,tkgd->skd/dot_general | solution.py:163
  432.5 7.1 %copy.63 = f32[3072,2,128]{2,1,0:T(2,128)} copy(f32[3072,2,128]{2,0,1:T(8,128)} %convolution_bitcast_fusion) | data formatting | bytes 6291456 | tf_op jit(solution)/shard_map/kgts,tkgd->skd/transpose | solution.py:163
  439.7 5.5 reshape_reshape.7
  445.1 4.4 all-to-all-start.3
  452.3 9.7 %multiply_reduce_fusion.1 = (f32[192,2,7]{0,2,1:T(8,128)S(1)}, bf16[192,2,7,128]{3,0,2,1:T(8,128)(2,1)}) fusion(bf16[192,2,7,128]{3,2,1,0:T(8,128)(2,1)} %reshape_squeeze.3, bf16[2,7,192,3072]{3,2,1,0:T(8,128)(2,1)} %copy-done.3, bf16[3072,2,128,1]{2,1,0,3:T(2,128)(2,1)S(1)} %bitcast.101), kind=kOutput, calls=%fused_computation.31 | convolution fusion | flops 2115646848 | bytes 19474944 | tf_op jit(solution)/shard_map/kgts,skd->tkgd/dot_general | solution.py:147
  461.9 14.0 %fusion.18 = f32[192,2,7,128]{3,0,2,1:T(8,128)} fusion(bf16[3072,2,128,1]{0,2,3,1:T(8,128)(2,1)} %bitcast.104, bf16[2,7,192,3072]{3,2,1,0:T(8,128)(2,1)} %copy-done.3, f32[2,7,192]{2,1,0:T(8,128)S(1)} %bitcast.111, bf16[3072,2,128,1]{2,1,0,3:T(2,128)(2,1)S(1)} %bitcast.102, bf16[192,2,7,128]{3,2,1,0:T(8,128)(2,1)} %reshape_squeeze.3), kind=kOutput, calls=%fused_computation.25 | convolution fusion | flops 4261232640 | bytes 21735936 | tf_op jit(solution)/shard_map/kgts,skd->tkgd/dot_general | solution.py:157
  482.9 5.1 all-to-all-done.3
  495.5 149.1 %all-reduce.4.cloned.1.call-done = (f32[3584,64]{0,1:T(8,128)}, f32[64,1792]{1,0:T(8,128)}, f32[3584,64]{0,1:T(8,128)}, f32[64,256]{1,0:T(8,128)}) async-done(((f32[3584,64]{0,1:T(8,128)}, f32[64,1792]{1,0:T(8,128)}, f32[3584,64]{0,1:T(8,128)}, f32[64,256]{1,0:T(8,128)}), (f32[3584,64]{0,1:T(8,128)}, f32[64,1792]{1,0:T(8,128)}, f32[3584,64]{0,1:T(8,128)}, f32[64,256]{1,0:T(8,128)})) %all-reduce.4.cloned.1.call-update) | async-done | bytes 2359312 | tf_op jit(solution)/shard_map/psum | solution.py:177
  (119 shorter events, 60.2 us)
Async XLA Ops:
  7.2 292.5 %copy-start = (bf16[3584,224]{0,1:T(8,128)(2,1)S(1)}, bf16[3584,224]{0,1:T(8,128)(2,1)}, u32[]{:S(2)}) copy-start(bf16[3584,224]{0,1:T(8,128)(2,1)} %param.26) | copy-start | bytes 4816900
  7.2 292.5 %all-gather.4.cloned.1.call-start = ((), (), s32[]{:S(2)}) async-start(), calls=%async_computation.4 | async-start | bytes 12386304 | tf_op jit(solution)/shard_map/all_gather | solution.py:100
  7.2 3.5 copy-start.5
  95.7 18.2 %copy-start.26 = (bf16[1,16,512]{2,1,0:T(8,128)(2,1)S(1)}, bf16[1,16,512]{2,1,0:T(8,128)(2,1)}, u32[]{:S(2)}) copy-start(bf16[1,16,512]{2,1,0:T(8,128)(2,1)} %param.19) | copy-start | bytes 49156
  113.9 54.9 %copy-start.9 = (bf16[1,192,3584]{2,1,0:T(8,128)(2,1)S(1)}, bf16[1,192,3584]{2,1,0:T(8,128)(2,1)}, u32[]{:S(2)}) copy-start(bf16[1,192,3584]{2,1,0:T(8,128)(2,1)} %param.24) | copy-start | bytes 4128772
  114.0 54.9 %copy-start.28 = (s32[1,192]{1,0:T(1,128)S(1)}, s32[1,192]{1,0:T(1,128)}, u32[]{:S(2)}) copy-start(s32[1,192]{1,0:T(1,128)} %param.33) | copy-start | bytes 2308
  171.1 135.8 %copy-start.22 = (bf16[3584,32]{0,1:T(8,128)(2,1)S(1)}, bf16[3584,32]{0,1:T(8,128)(2,1)}, u32[]{:S(2)}) copy-start(bf16[3584,32]{0,1:T(8,128)(2,1)} %param.27) | copy-start | bytes 688132
  299.7 7.3 %copy-start.2 = (bf16[1536,3584]{1,0:T(8,128)(2,1)S(1)}, bf16[1536,3584]{1,0:T(8,128)(2,1)}, u32[]{:S(2)}) copy-start(bf16[1536,3584]{1,0:T(8,128)(2,1)} %all-gather.4.cloned.1.call-done) | copy-start | bytes 33030148
  319.7 34.3 %all-to-all-start.2 = ((f32[8,192,288]{1,2,0:T(8,128)}), f32[8,192,288]{1,2,0:T(8,128)}, u32[]{:S(2)}, u32[]{:S(2)}) async-start(f32[8,192,288]{1,2,0:T(8,128)} %copy.45), calls=%async_computation.2 | async-start | bytes 4718592 | tf_op jit(solution)/shard_map/all_to_all | solution.py:109
  324.1 33.4 %copy-start.13 = (bf16[1,192,1792]{2,1,0:T(8,128)(2,1)S(1)}, bf16[1,192,1792]{2,1,0:T(8,128)(2,1)}, u32[]{:S(2)}) copy-start(bf16[1,192,1792]{2,1,0:T(8,128)(2,1)} %param.35) | copy-start | bytes 2064388
  324.1 65.0 %all-gather.8.cloned.1.call-start = ((), (), s32[]{:S(2)}) async-start(), calls=%async_computation.6 | async-start | bytes 1671168 | tf_op jit(solution)/shard_map/all_gather | solution.py:131
  355.8 4.7 copy-start.4
  355.8 4.7 copy-start.15
  356.6 93.0 %all-gather.6.cloned.1.call-start = ((), (), s32[]{:S(2)}) async-start(), calls=%async_computation.5 | async-start | bytes 1671168 | tf_op jit(solution)/shard_map/all_gather | solution.py:132
  357.5 3.5 copy-start.16
  361.0 4.5 copy-start.18
  390.8 19.7 %copy-start.8 = (bf16[3072,256]{0,1:T(8,128)(2,1)}, bf16[3072,256]{0,1:T(8,128)(2,1)S(1)}, u32[]{:S(2)}) copy-start(bf16[3072,256]{0,1:T(8,128)(2,1)S(1)} %copy.50) | copy-start | bytes 4718596
  410.5 13.3 %copy-start.6 = (bf16[192,2,7,128]{3,2,1,0:T(8,128)(2,1)S(1)}, bf16[192,2,7,128]{3,2,1,0:T(8,128)(2,1)}, u32[]{:S(2)}) copy-start(bf16[192,2,7,128]{3,2,1,0:T(8,128)(2,1)} %reshape_squeeze.3) | copy-start | bytes 2064388
  423.8 8.7 %copy-start.3 = (bf16[2,7,192,3072]{3,2,1,0:T(8,128)(2,1)}, bf16[2,7,192,3072]{3,2,1,0:T(8,128)(2,1)S(1)}, u32[]{:S(2)}) copy-start(bf16[2,7,192,3072]{3,2,1,0:T(8,128)(2,1)S(1)} %divide_convert_fusion) | copy-start | bytes 49545220
  445.1 42.8 %all-to-all-start.3 = ((f32[16,192,256]{2,1,0:T(8,128)}), f32[16,192,256]{2,1,0:T(8,128)}, u32[]{:S(2)}, u32[]{:S(2)}) async-start(f32[16,192,256]{2,1,0:T(8,128)} %reshape_reshape.7), calls=%async_computation.3 | async-start | bytes 6291456 | tf_op jit(solution)/shard_map/all_to_all | solution.py:22
  449.6 194.9 %all-reduce.4.cloned.1.call-start = ((), (), s32[]{:S(2)}) async-start(), calls=%async_computation.7 | async-start | bytes 4718592 | tf_op jit(solution)/shard_map/psum | solution.py:177
  482.9 7.2 %copy-start.21 = (bf16[192,64]{0,1:T(8,128)(2,1)S(1)}, bf16[192,64]{0,1:T(8,128)(2,1)}, u32[]{:S(2)}) copy-start(bf16[192,64]{0,1:T(8,128)(2,1)} %convolution_convert_fusion.3) | copy-start | bytes 73732
  482.9 8.0 %copy-start.24 = (bf16[64,256]{1,0:T(8,128)(2,1)S(1)}, bf16[64,256]{1,0:T(8,128)(2,1)}, u32[]{:S(2)}) copy-start(bf16[64,256]{1,0:T(8,128)(2,1)} %param.32) | copy-start | bytes 98308
  644.5 4.7 copy-start.1
  (11 other events, 23.4 us)
Sparse Core Ops, SparseCore 0:
  171.2 128.4 all-gather.3
  356.8 32.2 all-gather.7
  390.8 32.8 all-gather.5
  492.5 152.0 all-reduce.3
where the time goes:
time: 666 us; the launch traced here: 656 us
  waiting for transfers between devices  326 us (49%)
  blocking collectives  142 us (21%)
  matrix products  88.2 us (13%)
  local copies, waits for them, and re-layouts  48 us (7%)
  other arithmetic  27.9 us (4%)
  between operations  15.4 us (2%)
  starting transfers between devices  9.15 us (1%)
    psum x1, waiting for transfers between devices, on_device(): lax.psum((part_aq, part_bq, part_av, part_bv), ('gx', 'gy'))  149 us
    all_gather x1, waiting for transfers between devices, on_device(): slab_rows = lax.all_gather(normal, 'gy', axis=0, tiled=True)  129 us
    all_to_all x2, blocking collectives, sent_and_summed(): parts = lax.all_to_all(cut_along(array, dim, size), axis, 0, 0, tiled=True)  67.9 us
    psum x1, blocking collectives, on_device(): bridge = lax.psum(bridge_part, 'gx').astype(jnp.bfloat16)  52.2 us
    all_to_all x1, waiting for transfers between devices, on_device(): lax.all_to_all(projected, 'gy', split_axis=0, concat_axis=1, tiled=True)  29.3 us
    all_gather x1, blocking collectives, on_device(): lax.all_gather(hidden, 'gx', axis=0, tiled=True)  21.7 us
    sub x1, matrix products, on_device(): weights = jnp.exp(scores - row_max)  19.7 us
    dot_general x1, matrix products, on_device(): jnp.einsum('kgts,skd->tkgd', dscore, key_rows, preferred_element_type=jnp...  14 us
  transfers between devices with their start and end apart: 6, of which 5 were waited for; matrix products, arithmetic and copies ran while one was open for 17% of the time, Pallas kernels for 0%

commit v1 on v0

--- a/solution.py
+++ b/solution.py
@@ -9,6 +9,11 @@
 HD = 128
 rope_base = 1000000.0
 norm_eps = 1e-06
+
+
+def by_each_axis(value, axis_one, axis_two):
+    half = lax.psum(value, axis_one)
+    return lax.psum(half, axis_two)
 
 
 def cut_along(array, dim, size):
@@ -174,8 +179,8 @@
     ).astype(jnp.bfloat16)
     part_aq = jnp.einsum("td,tr->dr", normal, dlow_query, preferred_element_type=jnp.float32)
     part_av = jnp.einsum("td,tr->dr", normal, dlow_value, preferred_element_type=jnp.float32)
-    grad_aq, grad_bq, grad_av, grad_bv = lax.psum(
-        (part_aq, part_bq, part_av, part_bv), ("gx", "gy")
+    grad_aq, grad_bq, grad_av, grad_bv = by_each_axis(
+        (part_aq, part_bq, part_av, part_bv), "gx", "gy"
     )
     attn_out = attended.reshape(1, tokens, HEADS * HD)
     return (attn_out, grad_aq, grad_bq, grad_av, grad_bv)

time: 666 us -> 759 us (1.14)
  waiting for transfers between devices: 326 us -> 421 us
    psum x1 -> x2, waiting for transfers between devices: 149 us -> 244 us  [the longest x1 125 us: by_each_axis(): half = lax.psum(value, axis_one)]
  transfers between devices with their start and end apart: 6 -> 7, of which waited for: 5 -> 6; matrix products, arithmetic and copies ran while one was open for 17% -> 15% of each run, Pallas kernels for 0% -> 0%
where the time goes in v1:
time: 759 us; the launch traced here: 750 us
  waiting for transfers between devices  421 us (55%)
  blocking collectives  142 us (19%)
  matrix products  87.9 us (12%)
  local copies, waits for them, and re-layouts  47 us (6%)
  other arithmetic  27.9 us (4%)
  between operations  15.3 us (2%)
  starting transfers between devices  9.19 us (1%)
    all_gather x1, waiting for transfers between devices, on_device(): slab_rows = lax.all_gather(normal, 'gy', axis=0, tiled=True)  129 us
    psum x1, waiting for transfers between devices, by_each_axis(): half = lax.psum(value, axis_one)  125 us
    psum x1, waiting for transfers between devices, by_each_axis(): return lax.psum(half, axis_two)  118 us
    all_to_all x2, blocking collectives, sent_and_summed(): parts = lax.all_to_all(cut_along(array, dim, size), axis, 0, 0, tiled=True)  67.9 us
    psum x1, blocking collectives, on_device(): bridge = lax.psum(bridge_part, 'gx').astype(jnp.bfloat16)  52.2 us
    all_to_all x1, waiting for transfers between devices, on_device(): lax.all_to_all(projected, 'gy', split_axis=0, concat_axis=1, tiled=True)  29.3 us
    all_gather x1, blocking collectives, on_device(): lax.all_gather(hidden, 'gx', axis=0, tiled=True)  21.7 us
    sub x1, matrix products, on_device(): weights = jnp.exp(scores - row_max)  19.7 us
  transfers between devices with their start and end apart: 7, of which 6 were waited for; matrix products, arithmetic and copies ran while one was open for 15% of the time, Pallas kernels for 0%

profile of v1, /device:TPU:1, one launch (start us, length us, event | category | flops | bytes accessed | tf_op | source)
XLA Modules:
  0.0 749.7 jit_solution(3756903414158784054)
XLA Ops:
  7.2 3.4 fusion.59
  13.9 5.3 copy.44
  19.2 52.4 %all_to_all.31 = f32[16,8,7392]{2,1,0:T(8,128)} all-to-all(f32[16,8,7392]{2,1,0:T(8,128)} %bitcast.99), channel_id=1, replica_groups=mesh['gx'=16,'gy'=8] {'gx'}, dimensions={0} | all-to-all | bytes 7569408 | tf_op jit(solution)/shard_map/all_to_all | solution.py:27
  74.0 21.7 %all_gather.12 = bf16[128,3696]{1,0:T(8,128)(2,1)S(1)} all-gather(bf16[8,3696]{1,0:T(8,128)(2,1)S(1)} %fusion.37), channel_id=1, replica_groups=mesh['gx'=16,'gy'=8] {'gx'}, dimensions={0}, use_global_device_ids=true | all-gather | bytes 1005312 | tf_op jit(solution)/shard_map/all_gather | solution.py:83
  98.5 15.4 %all_to_all.32 = f32[8,16,512]{2,1,0:T(8,128)S(1)} all-to-all(f32[8,16,512]{2,1,0:T(8,128)S(1)} %bitcast.105), channel_id=1, replica_groups=mesh['gx'=16,'gy'=8] {'gy'}, dimensions={0} | all-to-all | bytes 524288 | tf_op jit(solution)/shard_map/all_to_all | solution.py:27
  116.7 52.2 %all-reduce.9 = bf16[16,3584]{1,0:T(8,128)(2,1)S(1)} all-reduce(f32[16,3584]{1,0:T(8,128)S(1)} %fusion.46), channel_id=1, replica_groups=mesh['gx'=16,'gy'=8] {'gx'}, use_global_device_ids=true, to_apply=%region_2.3 | all-reduce | flops 57344 | bytes 344064 | tf_op jit(solution)/shard_map/psum | solution.py:90
  171.1 128.6 %all-gather.4.cloned.1.call-done = bf16[1536,3584]{1,0:T(8,128)(2,1)} async-done(((bf16[192,3584]{1,0:T(8,128)(2,1)}), bf16[1536,3584]{1,0:T(8,128)(2,1)}) %all-gather.4.cloned.1.call-update) | async-done | bytes 11010064 | tf_op jit(solution)/shard_map/all_gather | solution.py:105
  299.7 7.2 fusion.62
  310.3 3.3 fusion.64
  315.8 3.9 copy.45
  319.7 4.4 all-to-all-start.2
  324.8 29.3 %all-to-all-done.2 = f32[8,192,288]{1,2,0:T(8,128)} async-done(((f32[8,192,288]{1,2,0:T(8,128)}), f32[8,192,288]{1,2,0:T(8,128)}, u32[]{:S(2)}, u32[]{:S(2)}) %all-to-all-start.2) | async-done | bytes 1769504 | tf_op jit(solution)/shard_map/all_to_all | solution.py:114
  375.3 13.8 %all-gather.8.cloned.1.call-done = bf16[3072,256]{1,0:T(8,128)(2,1)} async-done(((bf16[192,256]{1,0:T(8,128)(2,1)}), bf16[3072,256]{1,0:T(8,128)(2,1)}) %all-gather.8.cloned.1.call-update) | async-done | bytes 1572880 | tf_op jit(solution)/shard_map/all_gather | solution.py:136
  390.8 19.7 %fusion.58 = (f32[2,7,192]{2,1,0:T(8,128)S(1)}, f32[2,7,192,3072]{3,2,1,0:T(8,128)}) fusion(bf16[3072,2,128,1]{0,2,3,1:T(8,128)(2,1)S(1)} %bitcast.103, pred[192,3072]{1,0:T(8,128)(4,1)} %fusion.14, bf16[192,2,7,64]{3,0,2,1:T(8,128)(2,1)} %get-tuple-element.14, bf16[192,2,7,64]{3,0,2,1:T(8,128)(2,1)} %get-tuple-element.13), kind=kOutput, calls=%fused_computation.78 | convolution fusion | flops 2148338688 | bytes 35891712 | tf_op jit(solution)/shard_map/sub | solution.py:150
  410.5 13.3 %divide_convert_fusion = bf16[2,7,192,3072]{3,2,1,0:T(8,128)(2,1)S(1)} fusion(f32[2,7,192,3072]{3,2,1,0:T(8,128)} %get-tuple-element.29, f32[2,7,192]{2,1,0:T(8,128)S(1)} %get-tuple-element.28), kind=kLoop, calls=%fused_computation.5 | loop fusion | flops 16515072 | bytes 49555968 | tf_op jit(solution)/shard_map/convert_element_type | solution.py:151
  423.9 8.7 %convolution_bitcast_fusion = f32[3072,2,128]{2,0,1:T(8,128)} fusion(bf16[2,7,192,3072]{3,2,1,0:T(8,128)(2,1)S(1)} %divide_convert_fusion, bf16[192,2,7,128]{3,2,1,0:T(8,128)(2,1)S(1)} %copy-done.6), kind=kOutput, calls=%fused_computation.16 | convolution fusion | flops 2113929216 | bytes 20348928 | tf_op jit(solution)/shard_map/kgts,tkgd->skd/dot_general | solution.py:168
  432.5 7.1 copy.63
  439.7 5.5 reshape_reshape.7
  445.1 4.5 all-to-all-start.3
  452.3 9.7 %multiply_reduce_fusion.1 = (f32[192,2,7]{0,2,1:T(8,128)S(1)}, bf16[192,2,7,128]{3,0,2,1:T(8,128)(2,1)}) fusion(bf16[192,2,7,128]{3,2,1,0:T(8,128)(2,1)} %reshape_squeeze.3, bf16[2,7,192,3072]{3,2,1,0:T(8,128)(2,1)} %copy-done.3, bf16[3072,2,128,1]{2,1,0,3:T(2,128)(2,1)S(1)} %bitcast.101), kind=kOutput, calls=%fused_computation.31 | convolution fusion | flops 2115646848 | bytes 19474944 | tf_op jit(solution)/shard_map/kgts,skd->tkgd/dot_general | solution.py:152
  462.0 13.8 %fusion.18 = f32[192,2,7,128]{3,0,2,1:T(8,128)} fusion(bf16[3072,2,128,1]{0,2,3,1:T(8,128)(2,1)} %bitcast.104, bf16[2,7,192,3072]{3,2,1,0:T(8,128)(2,1)} %copy-done.3, f32[2,7,192]{2,1,0:T(8,128)S(1)} %bitcast.111, bf16[3072,2,128,1]{2,1,0,3:T(2,128)(2,1)S(1)} %bitcast.102, bf16[192,2,7,128]{3,2,1,0:T(8,128)(2,1)} %reshape_squeeze.3), kind=kOutput, calls=%fused_computation.25 | convolution fusion | flops 4261232640 | bytes 21735936 | tf_op jit(solution)/shard_map/kgts,skd->tkgd/dot_general | solution.py:162
  482.6 5.4 all-to-all-done.3
  492.4 125.4 %all-reduce.6.cloned.1.call-done = (f32[3584,64]{0,1:T(8,128)}, f32[64,1792]{1,0:T(8,128)}, f32[3584,64]{0,1:T(8,128)}, f32[64,256]{1,0:T(8,128)}) async-done(((f32[3584,64]{0,1:T(8,128)}, f32[64,1792]{1,0:T(8,128)}, f32[3584,64]{0,1:T(8,128)}, f32[64,256]{1,0:T(8,128)}), (f32[3584,64]{0,1:T(8,128)}, f32[64,1792]{1,0:T(8,128)}, f32[3584,64]{0,1:T(8,128)}, f32[64,256]{1,0:T(8,128)})) %all-reduce.6.cloned.1.call-update) | async-done | bytes 2359312 | tf_op jit(solution)/shard_map/psum | solution.py:15
  619.9 118.2 %all-reduce.8.cloned.1.call-done = (f32[3584,64]{0,1:T(8,128)}, f32[64,1792]{1,0:T(8,128)}, f32[3584,64]{0,1:T(8,128)}, f32[64,256]{1,0:T(8,128)}) async-done(((f32[3584,64]{0,1:T(8,128)}, f32[64,1792]{1,0:T(8,128)}, f32[3584,64]{0,1:T(8,128)}, f32[64,256]{1,0:T(8,128)}), (f32[3584,64]{0,1:T(8,128)}, f32[64,1792]{1,0:T(8,128)}, f32[3584,64]{0,1:T(8,128)}, f32[64,256]{1,0:T(8,128)})) %all-reduce.8.cloned.1.call-update) | async-done | bytes 2359312 | tf_op jit(solution)/shard_map/psum | solution.py:16
  (122 shorter events, 62.4 us)
Async XLA Ops:
  7.2 292.5 %copy-start = (bf16[3584,224]{0,1:T(8,128)(2,1)S(1)}, bf16[3584,224]{0,1:T(8,128)(2,1)}, u32[]{:S(2)}) copy-start(bf16[3584,224]{0,1:T(8,128)(2,1)} %param.26) | copy-start | bytes 4816900
  7.2 292.5 %all-gather.4.cloned.1.call-start = ((), (), s32[]{:S(2)}) async-start(), calls=%async_computation.4 | async-start | bytes 12386304 | tf_op jit(solution)/shard_map/all_gather | solution.py:105
  95.7 18.2 %copy-start.26 = (bf16[1,16,512]{2,1,0:T(8,128)(2,1)S(1)}, bf16[1,16,512]{2,1,0:T(8,128)(2,1)}, u32[]{:S(2)}) copy-start(bf16[1,16,512]{2,1,0:T(8,128)(2,1)} %param.19) | copy-start | bytes 49156
  113.9 54.9 %copy-start.9 = (bf16[1,192,3584]{2,1,0:T(8,128)(2,1)S(1)}, bf16[1,192,3584]{2,1,0:T(8,128)(2,1)}, u32[]{:S(2)}) copy-start(bf16[1,192,3584]{2,1,0:T(8,128)(2,1)} %param.24) | copy-start | bytes 4128772
  113.9 54.9 %copy-start.28 = (s32[1,192]{1,0:T(1,128)S(1)}, s32[1,192]{1,0:T(1,128)}, u32[]{:S(2)}) copy-start(s32[1,192]{1,0:T(1,128)} %param.33) | copy-start | bytes 2308
  171.1 135.8 %copy-start.22 = (bf16[3584,32]{0,1:T(8,128)(2,1)S(1)}, bf16[3584,32]{0,1:T(8,128)(2,1)}, u32[]{:S(2)}) copy-start(bf16[3584,32]{0,1:T(8,128)(2,1)} %param.27) | copy-start | bytes 688132
  299.7 7.3 copy-start.2
  319.7 34.3 %all-to-all-start.2 = ((f32[8,192,288]{1,2,0:T(8,128)}), f32[8,192,288]{1,2,0:T(8,128)}, u32[]{:S(2)}, u32[]{:S(2)}) async-start(f32[8,192,288]{1,2,0:T(8,128)} %copy.45), calls=%async_computation.2 | async-start | bytes 4718592 | tf_op jit(solution)/shard_map/all_to_all | solution.py:114
  324.1 33.4 %copy-start.13 = (bf16[1,192,1792]{2,1,0:T(8,128)(2,1)S(1)}, bf16[1,192,1792]{2,1,0:T(8,128)(2,1)}, u32[]{:S(2)}) copy-start(bf16[1,192,1792]{2,1,0:T(8,128)(2,1)} %param.35) | copy-start | bytes 2064388
  324.1 65.0 %all-gather.8.cloned.1.call-start = ((), (), s32[]{:S(2)}) async-start(), calls=%async_computation.6 | async-start | bytes 1671168 | tf_op jit(solution)/shard_map/all_gather | solution.py:136
  355.8 4.7 copy-start.4
  355.8 4.7 copy-start.15
  356.6 93.0 %all-gather.6.cloned.1.call-start = ((), (), s32[]{:S(2)}) async-start(), calls=%async_computation.5 | async-start | bytes 1671168 | tf_op jit(solution)/shard_map/all_gather | solution.py:137
  361.0 4.5 copy-start.18
  390.8 19.7 %copy-start.8 = (bf16[3072,256]{0,1:T(8,128)(2,1)}, bf16[3072,256]{0,1:T(8,128)(2,1)S(1)}, u32[]{:S(2)}) copy-start(bf16[3072,256]{0,1:T(8,128)(2,1)S(1)} %copy.50) | copy-start | bytes 4718596
  410.5 13.3 %copy-start.6 = (bf16[192,2,7,128]{3,2,1,0:T(8,128)(2,1)S(1)}, bf16[192,2,7,128]{3,2,1,0:T(8,128)(2,1)}, u32[]{:S(2)}) copy-start(bf16[192,2,7,128]{3,2,1,0:T(8,128)(2,1)} %reshape_squeeze.3) | copy-start | bytes 2064388
  423.8 8.7 %copy-start.3 = (bf16[2,7,192,3072]{3,2,1,0:T(8,128)(2,1)}, bf16[2,7,192,3072]{3,2,1,0:T(8,128)(2,1)S(1)}, u32[]{:S(2)}) copy-start(bf16[2,7,192,3072]{3,2,1,0:T(8,128)(2,1)S(1)} %divide_convert_fusion) | copy-start | bytes 49545220
  445.1 42.8 %all-to-all-start.3 = ((f32[16,192,256]{2,1,0:T(8,128)}), f32[16,192,256]{2,1,0:T(8,128)}, u32[]{:S(2)}, u32[]{:S(2)}) async-start(f32[16,192,256]{2,1,0:T(8,128)} %reshape_reshape.7), calls=%async_computation.3 | async-start | bytes 6291456 | tf_op jit(solution)/shard_map/all_to_all | solution.py:27
  449.6 168.2 %all-reduce.6.cloned.1.call-start = ((), (), s32[]{:S(2)}) async-start(), calls=%async_computation.7 | async-start | bytes 4718592 | tf_op jit(solution)/shard_map/psum | solution.py:15
  482.6 7.5 copy-start.21
  482.6 8.3 %copy-start.24 = (bf16[64,256]{1,0:T(8,128)(2,1)S(1)}, bf16[64,256]{1,0:T(8,128)(2,1)}, u32[]{:S(2)}) copy-start(bf16[64,256]{1,0:T(8,128)(2,1)} %param.32) | copy-start | bytes 98308
  492.4 125.5 %copy-start.7 = (bf16[192,2,7,128]{3,0,2,1:T(8,128)(2,1)S(1)}, bf16[192,2,7,128]{3,0,2,1:T(8,128)(2,1)}, u32[]{:S(2)}) copy-start(bf16[192,2,7,128]{3,0,2,1:T(8,128)(2,1)} %get-tuple-element.31) | copy-start | bytes 2064388
  492.4 245.7 %all-reduce.8.cloned.1.call-start = ((), (), s32[]{:S(2)}) async-start(), calls=%async_computation.8 | async-start | bytes 4718592 | tf_op jit(solution)/shard_map/psum | solution.py:16
  738.1 4.7 copy-start.1
  (12 other events, 29.3 us)
Sparse Core Ops, SparseCore 0:
  171.2 128.4 all-gather.3
  356.8 32.2 all-gather.7
  390.8 32.8 all-gather.5
  492.5 125.3 all-reduce.5
  620.5 117.5 all-reduce.7
